TPU v7x, 128 devices: a whole 4x4x4 slice. The times are simulated.
128 devices in a mesh: rows: 8 (over z, core), cols: 4 (over y), slabs: 4 (over x).
Axes of the slice: x: 4, y: 4, z: 4, core: 2. Of those that a mesh axis runs over, the one named last changes fastest.
Arguments:
- tracer: float32 [32, 256, 384, 128], P('rows', 'cols', 'slabs'), may hold values from 0.2 to 1.8
- crowding: float32 [32, 256, 384, 128], P('rows', 'cols', 'slabs'), may hold values from 0.5 to 2
Outputs:
- tracer_end: float32 [32, 256, 384, 128], P('rows', 'cols', 'slabs')
All inputs are finite; a program needn't handle non-finite values.
Results may differ from a plain program's by a relative error of at most 0.00002.
Values sent between devices are 32-bit elements.
A program may use at most 448 MiB of HBM per device.

v0:
```python
import jax
import jax.numpy as jnp
from jax import lax
from jax.sharding import PartitionSpec as P

STEPS = 4


def extended(shard, sides, width):
    edges = {}
    for axis, dim in sides:
        size, length = (lax.axis_size(axis), shard.shape[dim])
        up = [(i, (i + 1) % size) for i in range(size - 1)]
        last = lax.slice_in_dim(shard, length - width, length, axis=dim)
        first = lax.slice_in_dim(shard, 0, width, axis=dim)
        edges[dim] = (
            lax.ppermute(last, axis, up),
            lax.ppermute(first, axis, [(b, a) for a, b in up]),
        )
    done = []
    for _, dim in sides:
        low, high = edges[dim]
        around = [(width, width) if d in done else (0, 0) for d in range(shard.ndim)]
        shard = jnp.concatenate([jnp.pad(low, around), shard, jnp.pad(high, around)], axis=dim)
        done.append(dim)
    return shard


def inner_cells(values, dims):
    for dim in dims:
        values = lax.slice_in_dim(values, 1, values.shape[dim] - 1, axis=dim)
    return values


def side_cells(values, dim, start, dims):
    others = [other for other in dims if other != dim]
    values = inner_cells(values, others)
    return lax.slice_in_dim(values, start, start + values.shape[dim] - 2, axis=dim)


def advance(padded, crowding):
    middle = inner_cells(padded, (0, 1, 2))
    lower = [side_cells(padded, dim, 0, (0, 1, 2)) for dim in (0, 1, 2)]
    upper = [side_cells(padded, dim, 2, (0, 1, 2)) for dim in (0, 1, 2)]
    spread = lower[0] + upper[0] + lower[1] + upper[1] + lower[2] + upper[2] - 6.0 * middle
    return middle + 0.1 * spread + 0.2 * middle * (1.0 - middle * crowding)


def on_device(tracer, crowding):
    for step in range(STEPS):
        padded = extended(tracer, (("rows", 0), ("cols", 1), ("slabs", 2)), 1)
        tracer = advance(padded, crowding)
    return tracer


def solution(mesh):
    placed = (P("rows", "cols", "slabs", None), P("rows", "cols", "slabs", None))
    return jax.shard_map(
        on_device,
        mesh=mesh,
        in_specs=placed,
        out_specs=P("rows", "cols", "slabs", None),
        check_vma=False,
    )
```

profile of v0, /device:TPU:1, one launch (start us, length us, event | category | flops | bytes accessed | tf_op | source)
XLA Modules:
  0.0 376.0 jit_solution(5468073411313817603)
XLA Ops:
  0.0 5.0 %fusion.55 = (f32[1,64,96,128]{3,2,1,0:T(8,128)}, f32[1,64,96,128]{3,2,1,0:T(8,128)S(1)}) fusion(f32[4,64,96,128]{3,2,1,0:T(8,128)} %param.2), kind=kLoop, calls=%fused_computation.124 | loop fusion | bytes 12582912 | tf_op jit(solution)/shard_map/slice | solution.py:15
  5.0 4.9 %collective-permute-start = (f32[1,64,96,128]{3,2,1,0:T(8,128)S(1)}, f32[1,64,96,128]{3,2,1,0:T(8,128)S(1)}, u32[]{:S(2)}, u32[]{:S(2)}) collective-permute-start(f32[1,64,96,128]{3,2,1,0:T(8,128)S(1)} %get-tuple-element.28), channel_id=1, source_target_pairs={{0,16},{16,32},{32,48},{48,64},{64,80},{80,96},{96,112},{1,17},{17... | collective-permute-start | bytes 9437192 | tf_op jit(solution)/shard_map/ppermute | solution.py:17
  9.9 1.9 collective-permute-start.1
  11.8 1.1 fusion.54
  12.9 3.2 collective-permute-start.2
  16.1 1.3 collective-permute-start.3
  17.4 2.4 fusion.53
  19.8 3.8 %collective-permute-start.4 = (f32[4,64,1,128]{3,1,2,0:T(8,128)}, f32[4,64,1,128]{3,1,2,0:T(8,128)}, u32[]{:S(2)}, u32[]{:S(2)}) collective-permute-start(f32[4,64,1,128]{3,1,2,0:T(8,128)} %bitcast.12), channel_id=1, source_target_pairs={{0,1},{1,2},{2,3},{4,5},{5,6},{6,7},{8,9},{9,10},{10,11},{12,13},{... | collective-permute-start | bytes 393224 | tf_op jit(solution)/shard_map/ppermute | solution.py:17
  23.6 1.3 collective-permute-start.5
  24.9 0.7 pad.51
  25.7 18.4 %collective-permute-done = f32[1,64,96,128]{3,2,1,0:T(8,128)S(1)} collective-permute-done((f32[1,64,96,128]{3,2,1,0:T(8,128)S(1)}, f32[1,64,96,128]{3,2,1,0:T(8,128)S(1)}, u32[]{:S(2)}, u32[]{:S(2)}) %collective-permute-start) | collective-permute-done | bytes 3145760 | tf_op jit(solution)/shard_map/ppermute | solution.py:17
  44.1 1.9 constant_dynamic-update-slice_fusion.2
  45.9 10.3 %constant_dynamic-update-slice_fusion.1 = f32[6,64,96,128]{3,2,1,0:T(8,128)} fusion(f32[6,64,96,128]{3,2,1,0:T(8,128)} %constant_dynamic-update-slice_fusion.2, f32[4,64,96,128]{3,2,1,0:T(8,128)} %param.2), kind=kLoop, calls=%fused_computation.111 | loop fusion | bytes 25165824
  56.2 1.7 copy-done
  57.9 1.9 constant_dynamic-update-slice_fusion
  59.8 40.8 %fusion.38 = f32[4,64,96,128]{3,2,1,0:T(8,128)} fusion(f32[4,64,96,128]{3,2,1,0:T(8,128)} %param.2, f32[4,64,1,128]{3,2,1,0:T(1,128)} %bitcast.15, f32[6,1,96,128]{3,2,1,0:T(8,128)} %pad.51, f32[6,64,96,128]{3,2,1,0:T(8,128)} %constant_dynamic-update-slice_fusion, f32[6,1,96,128]{3,2,1,0:T(8,128)S(1)} %pad.50, f32[4,64,1,128]{3,2,1,0:T(1,128)} %bitcast.13, ...), kind=kLoop, calls=%fused_computation.93 | loop fusion | flops 94371840 | bytes 63766528 | tf_op jit(solution)/shard_map/add | solution.py:46
  100.6 3.3 fusion.51
  103.9 4.4 %collective-permute-start.6 = (f32[1,64,96,128]{3,2,1,0:T(8,128)S(1)}, f32[1,64,96,128]{3,2,1,0:T(8,128)S(1)}, u32[]{:S(2)}, u32[]{:S(2)}) collective-permute-start(f32[1,64,96,128]{3,2,1,0:T(8,128)S(1)} %get-tuple-element.19), channel_id=1, source_target_pairs={{0,16},{16,32},{32,48},{48,64},{64,80},{80,96},{96,112},{1,17},{17... | collective-permute-start | bytes 9437192 | tf_op jit(solution)/shard_map/ppermute | solution.py:17
  108.3 1.9 collective-permute-start.7
  110.2 1.1 fusion.52
  111.3 3.2 collective-permute-start.8
  114.5 1.3 collective-permute-start.9
  115.8 1.7 fusion.50
  117.6 3.1 collective-permute-start.10
  120.7 1.5 collective-permute-start.11
  122.2 0.7 pad.55
  123.0 3.5 collective-permute-done.11
  126.4 16.1 %collective-permute-done.6 = f32[1,64,96,128]{3,2,1,0:T(8,128)S(1)} collective-permute-done((f32[1,64,96,128]{3,2,1,0:T(8,128)S(1)}, f32[1,64,96,128]{3,2,1,0:T(8,128)S(1)}, u32[]{:S(2)}, u32[]{:S(2)}) %collective-permute-start.6) | collective-permute-done | bytes 3145760 | tf_op jit(solution)/shard_map/ppermute | solution.py:17
  142.5 4.4 %collective-permute-done.7 = f32[1,64,96,128]{3,2,1,0:T(8,128)S(1)} collective-permute-done((f32[1,64,96,128]{3,2,1,0:T(8,128)S(1)}, f32[1,64,96,128]{3,2,1,0:T(8,128)S(1)}, u32[]{:S(2)}, u32[]{:S(2)}) %collective-permute-start.7) | collective-permute-done | bytes 3145760 | tf_op jit(solution)/shard_map/ppermute | solution.py:18
  146.9 1.6 copy-done.2
  148.5 45.2 %fusion.27 = f32[4,64,96,128]{3,2,1,0:T(8,128)} fusion(f32[4,64,96,128]{3,2,1,0:T(8,128)} %fusion.38, f32[4,64,1,128]{3,2,1,0:T(1,128)} %bitcast.20, f32[6,1,96,128]{3,2,1,0:T(8,128)} %pad.55, f32[6,1,96,128]{3,2,1,0:T(8,128)S(1)} %pad.54, f32[1,64,96,128]{3,2,1,0:T(8,128)} %copy-done.2, f32[1,64,96,128]{3,2,1,0:T(8,128)S(1)} %collective-permute-done.6, ...), kind=kLoop, calls=%fused_computation.64 | loop fusion | flops 119537664 | bytes 44892160 | tf_op jit(solution)/shard_map/add | solution.py:46
  193.7 3.3 fusion.48
  197.0 1.9 collective-permute-start.12
  199.0 2.6 collective-permute-start.13
  201.6 1.1 fusion.49
  202.6 3.2 collective-permute-start.14
  205.8 1.3 collective-permute-start.15
  207.1 1.7 fusion.47
  208.9 3.1 collective-permute-start.16
  212.0 1.3 collective-permute-start.17
  213.4 1.2 collective-permute-done.15
  214.5 0.8 pad.59
  215.3 3.7 collective-permute-done.17
  219.0 14.1 %collective-permute-done.12 = f32[1,64,96,128]{3,2,1,0:T(8,128)S(1)} collective-permute-done((f32[1,64,96,128]{3,2,1,0:T(8,128)S(1)}, f32[1,64,96,128]{3,2,1,0:T(8,128)S(1)}, u32[]{:S(2)}, u32[]{:S(2)}) %collective-permute-start.12) | collective-permute-done | bytes 3145760 | tf_op jit(solution)/shard_map/ppermute | solution.py:17
  233.1 4.7 %collective-permute-done.13 = f32[1,64,96,128]{3,2,1,0:T(8,128)S(1)} collective-permute-done((f32[1,64,96,128]{3,2,1,0:T(8,128)S(1)}, f32[1,64,96,128]{3,2,1,0:T(8,128)S(1)}, u32[]{:S(2)}, u32[]{:S(2)}) %collective-permute-start.13) | collective-permute-done | bytes 3145760 | tf_op jit(solution)/shard_map/ppermute | solution.py:18
  237.8 1.7 copy-done.3
  239.5 45.3 %fusion.16 = f32[4,64,96,128]{3,2,1,0:T(8,128)} fusion(f32[4,64,96,128]{3,2,1,0:T(8,128)} %fusion.27, f32[4,64,1,128]{3,2,1,0:T(1,128)} %bitcast.21, f32[6,1,96,128]{3,2,1,0:T(8,128)} %pad.59, f32[6,1,96,128]{3,2,1,0:T(8,128)S(1)} %pad.58, f32[1,64,96,128]{3,2,1,0:T(8,128)} %copy-done.3, f32[1,64,96,128]{3,2,1,0:T(8,128)S(1)} %collective-permute-done.12, ...), kind=kLoop, calls=%fused_computation.35 | loop fusion | flops 119537664 | bytes 44892160 | tf_op jit(solution)/shard_map/add | solution.py:46
  284.8 3.3 fusion.45
  288.1 1.9 collective-permute-start.18
  290.1 2.6 collective-permute-start.19
  292.7 1.1 fusion.46
  293.7 3.2 collective-permute-start.20
  297.0 1.3 collective-permute-start.21
  298.3 1.7 fusion.44
  300.0 1.3 collective-permute-start.23
  301.3 0.3 collective-permute-done.20
  301.6 4.0 %collective-permute-start.22 = (f32[4,64,1,128]{3,1,2,0:T(8,128)S(1)}, f32[4,64,1,128]{3,1,2,0:T(8,128)S(1)}, u32[]{:S(2)}, u32[]{:S(2)}) collective-permute-start(f32[4,64,1,128]{3,1,2,0:T(8,128)S(1)} %bitcast.22), channel_id=1, source_target_pairs={{0,1},{1,2},{2,3},{4,5},{5,6},{6,7},{8,9},{9,10},{10,11},{12,13},{... | collective-permute-start | bytes 393224 | tf_op jit(solution)/shard_map/ppermute | solution.py:17
  305.6 0.8 pad.63
  306.4 0.9 collective-permute-done.23
  307.3 0.9 collective-permute-done.22
  308.2 16.1 %collective-permute-done.18 = f32[1,64,96,128]{3,2,1,0:T(8,128)S(1)} collective-permute-done((f32[1,64,96,128]{3,2,1,0:T(8,128)S(1)}, f32[1,64,96,128]{3,2,1,0:T(8,128)S(1)}, u32[]{:S(2)}, u32[]{:S(2)}) %collective-permute-start.18) | collective-permute-done | bytes 3145760 | tf_op jit(solution)/shard_map/ppermute | solution.py:17
  324.3 4.4 %collective-permute-done.19 = f32[1,64,96,128]{3,2,1,0:T(8,128)S(1)} collective-permute-done((f32[1,64,96,128]{3,2,1,0:T(8,128)S(1)}, f32[1,64,96,128]{3,2,1,0:T(8,128)S(1)}, u32[]{:S(2)}, u32[]{:S(2)}) %collective-permute-start.19) | collective-permute-done | bytes 3145760 | tf_op jit(solution)/shard_map/ppermute | solution.py:18
  328.7 1.6 copy-done.1
  330.3 45.5 %fusion.5 = f32[4,64,96,128]{3,2,1,0:T(8,128)} fusion(f32[4,64,96,128]{3,2,1,0:T(8,128)} %fusion.16, f32[4,64,1,128]{3,2,1,0:T(1,128)} %bitcast.16, f32[6,1,96,128]{3,2,1,0:T(8,128)} %pad.63, f32[6,1,96,128]{3,2,1,0:T(8,128)S(1)} %pad.62, f32[1,64,96,128]{3,2,1,0:T(8,128)} %copy-done.1, f32[1,64,96,128]{3,2,1,0:T(8,128)S(1)} %collective-permute-done.18, ...), kind=kLoop, calls=%fused_computation.6 | loop fusion | flops 119537664 | bytes 44892160 | tf_op jit(solution)/shard_map/add | solution.py:46
  (31 shorter events, 0.2 us)
Async XLA Ops:
  5.0 39.1 %collective-permute-start = (f32[1,64,96,128]{3,2,1,0:T(8,128)S(1)}, f32[1,64,96,128]{3,2,1,0:T(8,128)S(1)}, u32[]{:S(2)}, u32[]{:S(2)}) collective-permute-start(f32[1,64,96,128]{3,2,1,0:T(8,128)S(1)} %get-tuple-element.28), channel_id=1, source_target_pairs={{0,16},{16,32},{32,48},{48,64},{64,80},{80,96},{96,112},{1,17},{17... | collective-permute-start | bytes 9437192 | tf_op jit(solution)/shard_map/ppermute | solution.py:17
  9.9 46.3 %collective-permute-start.1 = (f32[1,64,96,128]{3,2,1,0:T(8,128)}, f32[1,64,96,128]{3,2,1,0:T(8,128)S(1)}, u32[]{:S(2)}, u32[]{:S(2)}) collective-permute-start(f32[1,64,96,128]{3,2,1,0:T(8,128)} %get-tuple-element.27), channel_id=1, source_target_pairs={{16,0},{32,16},{48,32},{64,48},{80,64},{96,80},{112,96},{17,1},{33... | collective-permute-start | bytes 9437192 | tf_op jit(solution)/shard_map/ppermute | solution.py:18
  12.9 10.7 %collective-permute-start.2 = (f32[4,1,96,128]{3,2,1,0:T(8,128)S(1)}, f32[4,1,96,128]{3,2,1,0:T(8,128)S(1)}, u32[]{:S(2)}, u32[]{:S(2)}) collective-permute-start(f32[4,1,96,128]{3,2,1,0:T(8,128)S(1)} %get-tuple-element.25), channel_id=1, source_target_pairs={{0,4},{4,8},{8,12},{1,5},{5,9},{9,13},{2,6},{6,10},{10,14},{3,7},{... | collective-permute-start | bytes 589832 | tf_op jit(solution)/shard_map/ppermute | solution.py:17
  16.1 8.8 %collective-permute-start.3 = (f32[4,1,96,128]{3,2,1,0:T(8,128)S(1)}, f32[4,1,96,128]{3,2,1,0:T(8,128)S(1)}, u32[]{:S(2)}, u32[]{:S(2)}) collective-permute-start(f32[4,1,96,128]{3,2,1,0:T(8,128)S(1)} %get-tuple-element.26), channel_id=1, source_target_pairs={{4,0},{8,4},{12,8},{5,1},{9,5},{13,9},{6,2},{10,6},{14,10},{7,3},{... | collective-permute-start | bytes 589832 | tf_op jit(solution)/shard_map/ppermute | solution.py:18
  19.8 40.0 %collective-permute-start.4 = (f32[4,64,1,128]{3,1,2,0:T(8,128)}, f32[4,64,1,128]{3,1,2,0:T(8,128)}, u32[]{:S(2)}, u32[]{:S(2)}) collective-permute-start(f32[4,64,1,128]{3,1,2,0:T(8,128)} %bitcast.12), channel_id=1, source_target_pairs={{0,1},{1,2},{2,3},{4,5},{5,6},{6,7},{8,9},{9,10},{10,11},{12,13},{... | collective-permute-start | bytes 393224 | tf_op jit(solution)/shard_map/ppermute | solution.py:17
  23.6 36.2 %collective-permute-start.5 = (f32[4,64,1,128]{3,1,2,0:T(8,128)}, f32[4,64,1,128]{3,1,2,0:T(8,128)}, u32[]{:S(2)}, u32[]{:S(2)}) collective-permute-start(f32[4,64,1,128]{3,1,2,0:T(8,128)} %bitcast.14), channel_id=1, source_target_pairs={{1,0},{2,1},{3,2},{5,4},{6,5},{7,6},{9,8},{10,9},{11,10},{13,12},{... | collective-permute-start | bytes 393224 | tf_op jit(solution)/shard_map/ppermute | solution.py:18
  56.2 1.7 copy-start
  103.9 38.6 %collective-permute-start.6 = (f32[1,64,96,128]{3,2,1,0:T(8,128)S(1)}, f32[1,64,96,128]{3,2,1,0:T(8,128)S(1)}, u32[]{:S(2)}, u32[]{:S(2)}) collective-permute-start(f32[1,64,96,128]{3,2,1,0:T(8,128)S(1)} %get-tuple-element.19), channel_id=1, source_target_pairs={{0,16},{16,32},{32,48},{48,64},{64,80},{80,96},{96,112},{1,17},{17... | collective-permute-start | bytes 9437192 | tf_op jit(solution)/shard_map/ppermute | solution.py:17
  108.3 38.6 %collective-permute-start.7 = (f32[1,64,96,128]{3,2,1,0:T(8,128)S(1)}, f32[1,64,96,128]{3,2,1,0:T(8,128)S(1)}, u32[]{:S(2)}, u32[]{:S(2)}) collective-permute-start(f32[1,64,96,128]{3,2,1,0:T(8,128)S(1)} %get-tuple-element.20), channel_id=1, source_target_pairs={{16,0},{32,16},{48,32},{64,48},{80,64},{96,80},{112,96},{17,1},{33... | collective-permute-start | bytes 9437192 | tf_op jit(solution)/shard_map/ppermute | solution.py:18
  111.3 9.4 %collective-permute-start.8 = (f32[4,1,96,128]{3,2,1,0:T(8,128)S(1)}, f32[4,1,96,128]{3,2,1,0:T(8,128)S(1)}, u32[]{:S(2)}, u32[]{:S(2)}) collective-permute-start(f32[4,1,96,128]{3,2,1,0:T(8,128)S(1)} %get-tuple-element.21), channel_id=1, source_target_pairs={{0,4},{4,8},{8,12},{1,5},{5,9},{9,13},{2,6},{6,10},{10,14},{3,7},{... | collective-permute-start | bytes 589832 | tf_op jit(solution)/shard_map/ppermute | solution.py:17
  114.5 7.7 %collective-permute-start.9 = (f32[4,1,96,128]{3,2,1,0:T(8,128)S(1)}, f32[4,1,96,128]{3,2,1,0:T(8,128)S(1)}, u32[]{:S(2)}, u32[]{:S(2)}) collective-permute-start(f32[4,1,96,128]{3,2,1,0:T(8,128)S(1)} %get-tuple-element.22), channel_id=1, source_target_pairs={{4,0},{8,4},{12,8},{5,1},{9,5},{13,9},{6,2},{10,6},{14,10},{7,3},{... | collective-permute-start | bytes 589832 | tf_op jit(solution)/shard_map/ppermute | solution.py:18
  117.6 5.4 %collective-permute-start.10 = (f32[4,64,1,128]{3,1,2,0:T(8,128)S(1)}, f32[4,64,1,128]{3,1,2,0:T(8,128)S(1)}, u32[]{:S(2)}, u32[]{:S(2)}) collective-permute-start(f32[4,64,1,128]{3,1,2,0:T(8,128)S(1)} %bitcast.26), channel_id=1, source_target_pairs={{0,1},{1,2},{2,3},{4,5},{5,6},{6,7},{8,9},{9,10},{10,11},{12,13},{... | collective-permute-start | bytes 393224 | tf_op jit(solution)/shard_map/ppermute | solution.py:17
  120.7 5.7 %collective-permute-start.11 = (f32[4,64,1,128]{3,1,2,0:T(8,128)S(1)}, f32[4,64,1,128]{3,1,2,0:T(8,128)S(1)}, u32[]{:S(2)}, u32[]{:S(2)}) collective-permute-start(f32[4,64,1,128]{3,1,2,0:T(8,128)S(1)} %bitcast.23), channel_id=1, source_target_pairs={{1,0},{2,1},{3,2},{5,4},{6,5},{7,6},{9,8},{10,9},{11,10},{13,12},{... | collective-permute-start | bytes 393224 | tf_op jit(solution)/shard_map/ppermute | solution.py:18
  123.0 25.6 %copy-start.5 = (f32[4,64,1,128]{3,1,2,0:T(8,128)}, f32[4,64,1,128]{3,1,2,0:T(8,128)S(1)}, u32[]{:S(2)}) copy-start(f32[4,64,1,128]{3,1,2,0:T(8,128)S(1)} %collective-permute-done.10) | copy-start | bytes 393220
  126.4 22.1 %copy-start.8 = (f32[4,64,1,128]{3,1,2,0:T(8,128)}, f32[4,64,1,128]{3,1,2,0:T(8,128)S(1)}, u32[]{:S(2)}) copy-start(f32[4,64,1,128]{3,1,2,0:T(8,128)S(1)} %collective-permute-done.11) | copy-start | bytes 393220
  146.9 1.6 copy-start.2
  197.0 36.1 %collective-permute-start.12 = (f32[1,64,96,128]{3,2,1,0:T(8,128)S(1)}, f32[1,64,96,128]{3,2,1,0:T(8,128)S(1)}, u32[]{:S(2)}, u32[]{:S(2)}) collective-permute-start(f32[1,64,96,128]{3,2,1,0:T(8,128)S(1)} %get-tuple-element.13), channel_id=1, source_target_pairs={{0,16},{16,32},{32,48},{48,64},{64,80},{80,96},{96,112},{1,17},{17... | collective-permute-start | bytes 9437192 | tf_op jit(solution)/shard_map/ppermute | solution.py:17
  199.0 38.9 %collective-permute-start.13 = (f32[1,64,96,128]{3,2,1,0:T(8,128)S(1)}, f32[1,64,96,128]{3,2,1,0:T(8,128)S(1)}, u32[]{:S(2)}, u32[]{:S(2)}) collective-permute-start(f32[1,64,96,128]{3,2,1,0:T(8,128)S(1)} %get-tuple-element.14), channel_id=1, source_target_pairs={{16,0},{32,16},{48,32},{64,48},{80,64},{96,80},{112,96},{17,1},{33... | collective-permute-start | bytes 9437192 | tf_op jit(solution)/shard_map/ppermute | solution.py:18
  202.6 9.4 %collective-permute-start.14 = (f32[4,1,96,128]{3,2,1,0:T(8,128)S(1)}, f32[4,1,96,128]{3,2,1,0:T(8,128)S(1)}, u32[]{:S(2)}, u32[]{:S(2)}) collective-permute-start(f32[4,1,96,128]{3,2,1,0:T(8,128)S(1)} %get-tuple-element.15), channel_id=1, source_target_pairs={{0,4},{4,8},{8,12},{1,5},{5,9},{9,13},{2,6},{6,10},{10,14},{3,7},{... | collective-permute-start | bytes 589832 | tf_op jit(solution)/shard_map/ppermute | solution.py:17
  205.8 8.7 %collective-permute-start.15 = (f32[4,1,96,128]{3,2,1,0:T(8,128)S(1)}, f32[4,1,96,128]{3,2,1,0:T(8,128)S(1)}, u32[]{:S(2)}, u32[]{:S(2)}) collective-permute-start(f32[4,1,96,128]{3,2,1,0:T(8,128)S(1)} %get-tuple-element.16), channel_id=1, source_target_pairs={{4,0},{8,4},{12,8},{5,1},{9,5},{13,9},{6,2},{10,6},{14,10},{7,3},{... | collective-permute-start | bytes 589832 | tf_op jit(solution)/shard_map/ppermute | solution.py:18
  208.9 6.4 %collective-permute-start.16 = (f32[4,64,1,128]{3,1,2,0:T(8,128)S(1)}, f32[4,64,1,128]{3,1,2,0:T(8,128)S(1)}, u32[]{:S(2)}, u32[]{:S(2)}) collective-permute-start(f32[4,64,1,128]{3,1,2,0:T(8,128)S(1)} %bitcast.27), channel_id=1, source_target_pairs={{0,1},{1,2},{2,3},{4,5},{5,6},{6,7},{8,9},{9,10},{10,11},{12,13},{... | collective-permute-start | bytes 393224 | tf_op jit(solution)/shard_map/ppermute | solution.py:17
  212.0 7.0 %collective-permute-start.17 = (f32[4,64,1,128]{3,1,2,0:T(8,128)S(1)}, f32[4,64,1,128]{3,1,2,0:T(8,128)S(1)}, u32[]{:S(2)}, u32[]{:S(2)}) collective-permute-start(f32[4,64,1,128]{3,1,2,0:T(8,128)S(1)} %bitcast.24), channel_id=1, source_target_pairs={{1,0},{2,1},{3,2},{5,4},{6,5},{7,6},{9,8},{10,9},{11,10},{13,12},{... | collective-permute-start | bytes 393224 | tf_op jit(solution)/shard_map/ppermute | solution.py:18
  215.3 24.2 %copy-start.6 = (f32[4,64,1,128]{3,1,2,0:T(8,128)}, f32[4,64,1,128]{3,1,2,0:T(8,128)S(1)}, u32[]{:S(2)}) copy-start(f32[4,64,1,128]{3,1,2,0:T(8,128)S(1)} %collective-permute-done.16) | copy-start | bytes 393220
  219.0 20.5 %copy-start.9 = (f32[4,64,1,128]{3,1,2,0:T(8,128)}, f32[4,64,1,128]{3,1,2,0:T(8,128)S(1)}, u32[]{:S(2)}) copy-start(f32[4,64,1,128]{3,1,2,0:T(8,128)S(1)} %collective-permute-done.17) | copy-start | bytes 393220
  237.8 1.7 copy-start.3
  288.1 36.1 %collective-permute-start.18 = (f32[1,64,96,128]{3,2,1,0:T(8,128)S(1)}, f32[1,64,96,128]{3,2,1,0:T(8,128)S(1)}, u32[]{:S(2)}, u32[]{:S(2)}) collective-permute-start(f32[1,64,96,128]{3,2,1,0:T(8,128)S(1)} %get-tuple-element.7), channel_id=1, source_target_pairs={{0,16},{16,32},{32,48},{48,64},{64,80},{80,96},{96,112},{1,17},{17... | collective-permute-start | bytes 9437192 | tf_op jit(solution)/shard_map/ppermute | solution.py:17
  290.1 38.6 %collective-permute-start.19 = (f32[1,64,96,128]{3,2,1,0:T(8,128)S(1)}, f32[1,64,96,128]{3,2,1,0:T(8,128)S(1)}, u32[]{:S(2)}, u32[]{:S(2)}) collective-permute-start(f32[1,64,96,128]{3,2,1,0:T(8,128)S(1)} %get-tuple-element.8), channel_id=1, source_target_pairs={{16,0},{32,16},{48,32},{64,48},{80,64},{96,80},{112,96},{17,1},{33... | collective-permute-start | bytes 9437192 | tf_op jit(solution)/shard_map/ppermute | solution.py:18
  293.7 7.8 %collective-permute-start.20 = (f32[4,1,96,128]{3,2,1,0:T(8,128)S(1)}, f32[4,1,96,128]{3,2,1,0:T(8,128)S(1)}, u32[]{:S(2)}, u32[]{:S(2)}) collective-permute-start(f32[4,1,96,128]{3,2,1,0:T(8,128)S(1)} %get-tuple-element.9), channel_id=1, source_target_pairs={{0,4},{4,8},{8,12},{1,5},{5,9},{9,13},{2,6},{6,10},{10,14},{3,7},{... | collective-permute-start | bytes 589832 | tf_op jit(solution)/shard_map/ppermute | solution.py:17
  297.0 8.7 %collective-permute-start.21 = (f32[4,1,96,128]{3,2,1,0:T(8,128)S(1)}, f32[4,1,96,128]{3,2,1,0:T(8,128)S(1)}, u32[]{:S(2)}, u32[]{:S(2)}) collective-permute-start(f32[4,1,96,128]{3,2,1,0:T(8,128)S(1)} %get-tuple-element.10), channel_id=1, source_target_pairs={{4,0},{8,4},{12,8},{5,1},{9,5},{13,9},{6,2},{10,6},{14,10},{7,3},{... | collective-permute-start | bytes 589832 | tf_op jit(solution)/shard_map/ppermute | solution.py:18
  300.0 7.3 %collective-permute-start.23 = (f32[4,64,1,128]{3,1,2,0:T(8,128)S(1)}, f32[4,64,1,128]{3,1,2,0:T(8,128)S(1)}, u32[]{:S(2)}, u32[]{:S(2)}) collective-permute-start(f32[4,64,1,128]{3,1,2,0:T(8,128)S(1)} %bitcast.25), channel_id=1, source_target_pairs={{1,0},{2,1},{3,2},{5,4},{6,5},{7,6},{9,8},{10,9},{11,10},{13,12},{... | collective-permute-start | bytes 393224 | tf_op jit(solution)/shard_map/ppermute | solution.py:18
  301.6 6.6 %collective-permute-start.22 = (f32[4,64,1,128]{3,1,2,0:T(8,128)S(1)}, f32[4,64,1,128]{3,1,2,0:T(8,128)S(1)}, u32[]{:S(2)}, u32[]{:S(2)}) collective-permute-start(f32[4,64,1,128]{3,1,2,0:T(8,128)S(1)} %bitcast.22), channel_id=1, source_target_pairs={{0,1},{1,2},{2,3},{4,5},{5,6},{6,7},{8,9},{9,10},{10,11},{12,13},{... | collective-permute-start | bytes 393224 | tf_op jit(solution)/shard_map/ppermute | solution.py:17
  307.3 23.0 %copy-start.4 = (f32[4,64,1,128]{3,1,2,0:T(8,128)}, f32[4,64,1,128]{3,1,2,0:T(8,128)S(1)}, u32[]{:S(2)}) copy-start(f32[4,64,1,128]{3,1,2,0:T(8,128)S(1)} %collective-permute-done.23) | copy-start | bytes 393220
  308.2 22.1 %copy-start.7 = (f32[4,64,1,128]{3,1,2,0:T(8,128)}, f32[4,64,1,128]{3,1,2,0:T(8,128)S(1)}, u32[]{:S(2)}) copy-start(f32[4,64,1,128]{3,1,2,0:T(8,128)S(1)} %collective-permute-done.22) | copy-start | bytes 393220
  328.7 1.7 copy-start.1
where the time goes:
time: 377 us; the launch traced here: 376 us
  other arithmetic  177 us (47%)
  waiting for transfers between devices  88.6 us (24%)
  starting transfers between devices  59.5 us (16%)
  local copies, waits for them, and re-layouts  50.5 us (13%)
    add x4, other arithmetic, advance(): return middle + 0.1 * spread + 0.2 * middle * (1.0 - middle * crowding)  177 us
    ppermute x12, waiting for transfers between devices, extended(): lax.ppermute(last, axis, up)  65.8 us
    ppermute x12, starting transfers between devices, extended(): lax.ppermute(last, axis, up)  40 us
    ppermute x12, waiting for transfers between devices, extended(): lax.ppermute(first, axis, [(b, a) for a, b in up])  22.8 us
    slice x11, local copies, waits for them, and re-layouts, extended(): last = lax.slice_in_dim(shard, length - width, length, axis=dim)  21.8 us
    ppermute x12, starting transfers between devices, extended(): lax.ppermute(first, axis, [(b, a) for a, b in up])  19.6 us
    unnamed x22, local copies, waits for them, and re-layouts  18.8 us
  transfers between devices with their start and end apart: 24, of which 14 were waited for; matrix products, arithmetic and copies ran while one was open for 8% of the time, Pallas kernels for 0%

commit v1 on v0

v1 whole, which is shorter than its diff:
```python
import functools

import jax
import jax.numpy as jnp
from jax import lax
from jax.experimental import pallas as pl
from jax.experimental.pallas import tpu as pltpu
from jax.sharding import PartitionSpec as P

STEPS = 4
CHUNKS = 8
MESH = pl.DeviceIdType.MESH
VMEM_LIMIT = 48 * 1024 * 1024


def kernel(sizes, tracer, crowding, out, field, far_in, near_in, slab_in, slab_out,
           load_sem, far_send, far_recv, near_send, near_recv,
           cols_send, cols_recv, slab_send, slab_recv):
    layers, lines, depth, _ = tracer.shape
    per_chunk = lines // CHUNKS
    tiles = depth // 8
    rows_n, cols_n, slabs_n = sizes
    r, q, s = lax.axis_index("rows"), lax.axis_index("cols"), lax.axis_index("slabs")
    core = lax.rem(r, 2)
    step_up = 1 - 2 * core
    first = (layers - 1) * core

    def layer(d):
        return first + step_up * d

    far_row = r - step_up
    near_row = r + step_up
    has_far = jnp.logical_and(far_row >= 0, far_row < rows_n)
    around = (
        ("cols", q, cols_n),
        ("slabs", s, slabs_n),
    )

    loads = [
        pltpu.make_async_copy(tracer, field.at[0, :, pl.ds(1, lines)], load_sem.at[0]),
        pltpu.make_async_copy(crowding, out, load_sem.at[1]),
    ]
    loads[0].start()

    barrier = pltpu.get_barrier_semaphore()
    greeted = jnp.int32(1)
    pl.semaphore_signal(barrier, inc=1, device_id={"rows": near_row}, device_id_type=MESH)

    @pl.when(has_far)
    def _():
        pl.semaphore_signal(barrier, inc=1, device_id={"rows": far_row}, device_id_type=MESH)

    greeted = greeted + has_far.astype(jnp.int32)
    for axis, me, n in around:
        @pl.when(me > 0)
        def _():
            pl.semaphore_signal(barrier, inc=1, device_id={axis: me - 1}, device_id_type=MESH)

        @pl.when(me < n - 1)
        def _():
            pl.semaphore_signal(barrier, inc=1, device_id={axis: me + 1}, device_id_type=MESH)

        greeted = greeted + (me > 0).astype(jnp.int32) + (me < n - 1).astype(jnp.int32)
    pl.semaphore_wait(barrier, greeted)

    def far_copy(par, c, source):
        part = pl.ds(c * per_chunk, per_chunk)
        return pltpu.make_async_remote_copy(
            src_ref=source, dst_ref=far_in.at[par, part],
            send_sem=far_send.at[par, c], recv_sem=far_recv.at[par, c],
            device_id={"rows": far_row}, device_id_type=MESH,
        )

    def far_source(par, c):
        return field.at[par, layer(0), pl.ds(1 + c * per_chunk, per_chunk)]

    def near_copy(par, source):
        return pltpu.make_async_remote_copy(
            src_ref=source, dst_ref=near_in.at[par],
            send_sem=near_send.at[par], recv_sem=near_recv.at[par],
            device_id={"rows": near_row}, device_id_type=MESH,
        )

    def near_source(par):
        return field.at[par, layer(layers - 1), pl.ds(1, lines)]

    def cols_copy(par, side, source):
        return pltpu.make_async_remote_copy(
            src_ref=source, dst_ref=field.at[par, :, (lines + 1) * (1 - side)],
            send_sem=cols_send.at[par, side], recv_sem=cols_recv.at[par, side],
            device_id={"cols": q - 1 + 2 * side}, device_id_type=MESH,
        )

    def cols_source(par, side):
        return field.at[par, :, 1 + (lines - 1) * side]

    def slab_copy(par, side):
        return pltpu.make_async_remote_copy(
            src_ref=slab_out.at[par, side], dst_ref=slab_in.at[par, 1 - side],
            send_sem=slab_send.at[par, side], recv_sem=slab_recv.at[par, side],
            device_id={"slabs": s - 1 + 2 * side}, device_id_type=MESH,
        )

    def has(me, n, side):
        return me > 0 if side == 0 else me < n - 1

    @pl.when(has_far)
    def _():
        @pl.loop(0, CHUNKS)
        def _(c):
            far_copy(0, c, tracer.at[layer(0), pl.ds(c * per_chunk, per_chunk)]).start()

    near_copy(0, tracer.at[layer(layers - 1)]).start()
    for side in (0, 1):
        @pl.when(has(q, cols_n, side))
        def _():
            cols_copy(0, side, tracer.at[:, (lines - 1) * side]).start()
    loads[1].start()

    for side in (0, 1):
        @pl.when(jnp.logical_not(has(q, cols_n, side)))
        def _():
            for par in (0, 1):
                field[par, :, (lines + 1) * side] = jnp.zeros((layers, depth, 128), jnp.float32)

        @pl.when(jnp.logical_not(has(s, slabs_n, side)))
        def _():
            for par in (0, 1):
                @pl.loop(0, layers)
                def _(i):
                    slab_in[par, side, i] = jnp.zeros((lines, 128), jnp.float32)

    @pl.when(jnp.logical_not(has_far))
    def _():
        for par in (0, 1):
            @pl.loop(0, lines)
            def _(j):
                far_in[par, j] = jnp.zeros((depth, 128), jnp.float32)

    loads[0].wait()

    @pl.loop(0, layers)
    def _(i):
        @pl.loop(0, lines)
        def _(j):
            slab_out[0, 0, i, pl.ds(j, 1), :] = field[0, i, j + 1, 0:1, :]
            slab_out[0, 1, i, pl.ds(j, 1), :] = field[0, i, j + 1, depth - 1:depth, :]

    for side in (0, 1):
        @pl.when(has(s, slabs_n, side))
        def _():
            slab_copy(0, side).start()
    loads[1].wait()

    row = lax.broadcasted_iota(jnp.int32, (8, 128), 0)

    def advance(t, d, start, count):
        par, last = t % 2, t == STEPS - 1
        here = layer(d)

        @pl.loop(start, start + count)
        def _(j):
            below = slab_in[par, 0, here, pl.ds(j, 1), :]
            above = slab_in[par, 1, here, pl.ds(j, 1), :]
            for k in range(tiles):
                part = pl.ds(8 * k, 8)
                mid = field[par, here, j + 1, part, :]
                if k == 0:
                    lower = jnp.where(row == 0, below, pltpu.roll(mid, 1, 0))
                else:
                    lower = field[par, here, j + 1, pl.ds(8 * k - 1, 8), :]
                if k == tiles - 1:
                    upper = jnp.where(row == 7, above, pltpu.roll(mid, 7, 0))
                else:
                    upper = field[par, here, j + 1, pl.ds(8 * k + 1, 8), :]
                outer = far_in[par, j, part, :] if d == 0 else field[par, layer(d - 1), j + 1, part, :]
                inner = near_in[par, j, part, :] if d == layers - 1 else field[par, layer(d + 1), j + 1, part, :]
                spread = (
                    (lower + upper)
                    + (field[par, here, j, part, :] + field[par, here, j + 2, part, :])
                    + (outer + inner)
                )
                crowd = out[here, j, part, :]
                new = 0.1 * spread + mid * (0.6 - 0.2 * (mid * crowd))
                if last:
                    out[here, j, part, :] = new
                else:
                    field[1 - par, here, j + 1, part, :] = new
                    if k == 0:
                        slab_out[1 - par, 0, here, pl.ds(j, 1), :] = new[0:1]
                    if k == tiles - 1:
                        slab_out[1 - par, 1, here, pl.ds(j, 1), :] = new[7:8]

    for t in range(STEPS):
        par, last = t % 2, t == STEPS - 1
        nxt = 1 - par
        near_copy(par, near_source(par)).wait_recv()
        for side in (0, 1):
            @pl.when(has(q, cols_n, 1 - side))
            def _():
                cols_copy(par, side, cols_source(par, side)).wait_recv()

            @pl.when(has(s, slabs_n, 1 - side))
            def _():
                slab_copy(par, side).wait_recv()
        if t > 0:
            near_copy(nxt, near_source(nxt)).wait_send()
            for side in (0, 1):
                @pl.when(has(q, cols_n, side))
                def _():
                    cols_copy(nxt, side, cols_source(nxt, side)).wait_send()

                @pl.when(has(s, slabs_n, side))
                def _():
                    slab_copy(nxt, side).wait_send()
        for d in range(layers - 1, 0, -1):
            advance(t, d, 0, lines)
        if not last:
            near_copy(nxt, near_source(nxt)).start()

        @pl.loop(0, CHUNKS)
        def _(c):
            @pl.when(has_far)
            def _():
                far_copy(par, c, far_source(par, c)).wait_recv()
                if t > 0:
                    far_copy(nxt, c, far_source(nxt, c)).wait_send()

            advance(t, 0, c * per_chunk, per_chunk)
            if not last:
                @pl.when(has_far)
                def _():
                    far_copy(nxt, c, far_source(nxt, c)).start()
        if not last:
            for side in (0, 1):
                @pl.when(has(q, cols_n, side))
                def _():
                    cols_copy(nxt, side, cols_source(nxt, side)).start()

                @pl.when(has(s, slabs_n, side))
                def _():
                    slab_copy(nxt, side).start()

    par = (STEPS - 1) % 2
    near_copy(par, near_source(par)).wait_send()
    for side in (0, 1):
        @pl.when(has(q, cols_n, side))
        def _():
            cols_copy(par, side, cols_source(par, side)).wait_send()

        @pl.when(has(s, slabs_n, side))
        def _():
            slab_copy(par, side).wait_send()

    @pl.when(has_far)
    def _():
        @pl.loop(0, CHUNKS)
        def _(c):
            far_copy(par, c, far_source(par, c)).wait_send()


def solution(mesh):
    sizes = tuple(mesh.shape[axis] for axis in ("rows", "cols", "slabs"))

    def on_device(tracer, crowding):
        layers, lines, depth, lanes = tracer.shape
        dma = pltpu.SemaphoreType.DMA
        return pl.pallas_call(
            functools.partial(kernel, sizes),
            out_shape=pltpu.VMEM(tracer.shape, jnp.float32),
            in_specs=[pl.BlockSpec(memory_space=pl.ANY)] * 2,
            out_specs=pl.BlockSpec(memory_space=pltpu.VMEM),
            scratch_shapes=[
                pltpu.VMEM((2, layers, lines + 2, depth, lanes), jnp.float32),
                pltpu.VMEM((2, lines, depth, lanes), jnp.float32),
                pltpu.VMEM((2, lines, depth, lanes), jnp.float32),
                pltpu.VMEM((2, 2, layers, lines, lanes), jnp.float32),
                pltpu.VMEM((2, 2, layers, lines, lanes), jnp.float32),
                dma((2,)),
                dma((2, CHUNKS)), dma((2, CHUNKS)),
                dma((2,)), dma((2,)),
                dma((2, 2)), dma((2, 2)),
                dma((2, 2)), dma((2, 2)),
            ],
            compiler_params=pltpu.CompilerParams(
                collective_id=0, has_side_effects=True, vmem_limit_bytes=VMEM_LIMIT,
            ),
        )(tracer, crowding)

    placed = P("rows", "cols", "slabs", None)
    return jax.shard_map(on_device, mesh=mesh, in_specs=(placed, placed), out_specs=placed, check_vma=False)
```

time: 377 us -> 147 us (0.39)
  other arithmetic: 177 us -> 0 us
  Pallas kernels: 0 us -> 142 us
  waiting for transfers between devices: 88.6 us -> 0 us
  starting transfers between devices: 59.5 us -> 0 us
  local copies, waits for them, and re-layouts: 50.5 us -> 4.78 us
    add x4 -> x0, other arithmetic: 177 us -> none  [advance(): return middle + 0.1 * spread + 0.2 * middle * (1.0 - middle * crowding)]
    pallas_call x0 -> x1, Pallas kernels: none -> 142 us  [on_device(): pl.pallas_call(functools.partial(kernel, sizes), out_shape=pltpu.VMEM(tra...]
    ppermute x24 -> x0, waiting for transfers between devices: 88.6 us -> none  [the longest x12 65.8 us: extended(): lax.ppermute(last, axis, up)]
    ppermute x24 -> x0, starting transfers between devices: 59.5 us -> none  [the longest x12 40 us: extended(): lax.ppermute(last, axis, up)]
    slice x12 -> x0, local copies, waits for them, and re-layouts: 26.7 us -> none  [the longest x11 21.8 us: extended(): last = lax.slice_in_dim(shard, length - width, length, axis=dim)]
    unnamed x22 -> x1, local copies, waits for them, and re-layouts: 18.8 us -> 4.78 us
  transfers between devices with their start and end apart: 24 -> 0, of which waited for: 14 -> 0; matrix products, arithmetic and copies ran while one was open for 8% -> 0% of each run, Pallas kernels for 0% -> 0%
where the time goes in v1:
time: 147 us; the launch traced here: 146 us
  Pallas kernels  142 us (97%)
  local copies, waits for them, and re-layouts  4.78 us (3%)
    pallas_call x1, Pallas kernels, on_device(): pl.pallas_call(functools.partial(kernel, sizes), out_shape=pltpu.VMEM(tra...  142 us
    unnamed x1, local copies, waits for them, and re-layouts  4.78 us

profile of v1, /device:TPU:1, one launch (start us, length us, event | category | flops | bytes accessed | tf_op | source)
XLA Modules:
  0.0 146.4 jit_solution(6145627920124540283)
XLA Ops:
  0.0 141.7 %shard_map.28 = f32[4,64,96,128]{3,2,1,0:T(8,128)S(1)} custom-call(f32[4,64,96,128]{3,2,1,0:T(8,128)} %tracer.1, f32[4,64,96,128]{3,2,1,0:T(8,128)} %crowding.1), custom_call_target="tpu_custom_call" | custom-call | tf_op jit(solution)/shard_map/pallas_call | solution.py:268
  141.7 4.8 %copy.4 = f32[4,64,96,128]{3,2,1,0:T(8,128)} copy(f32[4,64,96,128]{3,2,1,0:T(8,128)S(1)} %shard_map.28) | data formatting | bytes 25165824

commit v2 on v1

--- a/solution.py
+++ b/solution.py
@@ -8,16 +8,16 @@
 from jax.sharding import PartitionSpec as P
 
 STEPS = 4
-CHUNKS = 8
+PARTS = ((32, 32), (32, 32), (32, 32), (32, 16, 8, 6, 2))
+MOST = max(map(len, PARTS))
 MESH = pl.DeviceIdType.MESH
 VMEM_LIMIT = 48 * 1024 * 1024
 
 
 def kernel(sizes, tracer, crowding, out, field, far_in, near_in, slab_in, slab_out,
-           load_sem, far_send, far_recv, near_send, near_recv,
+           all_in, load_sem, far_send, far_recv, near_send, near_recv,
            cols_send, cols_recv, slab_send, slab_recv):
     layers, lines, depth, _ = tracer.shape
-    per_chunk = lines // CHUNKS
     tiles = depth // 8
     rows_n, cols_n, slabs_n = sizes
     r, q, s = lax.axis_index("rows"), lax.axis_index("cols"), lax.axis_index("slabs")
@@ -36,43 +36,45 @@
         ("slabs", s, slabs_n),
     )
 
+    def spans(t):
+        start = 0
+        for p, count in enumerate(PARTS[t]):
+            yield p, start, count
+            start += count
+
     loads = [
         pltpu.make_async_copy(tracer, field.at[0, :, pl.ds(1, lines)], load_sem.at[0]),
         pltpu.make_async_copy(crowding, out, load_sem.at[1]),
     ]
-    loads[0].start()
 
     barrier = pltpu.get_barrier_semaphore()
-    greeted = jnp.int32(1)
-    pl.semaphore_signal(barrier, inc=1, device_id={"rows": near_row}, device_id_type=MESH)
-
-    @pl.when(has_far)
-    def _():
-        pl.semaphore_signal(barrier, inc=1, device_id={"rows": far_row}, device_id_type=MESH)
-
-    greeted = greeted + has_far.astype(jnp.int32)
+
+    def greet(there, target):
+        @pl.when(there)
+        def _():
+            pl.semaphore_signal(barrier, inc=1, device_id=target, device_id_type=MESH)
+
+    greet(has_far, {"rows": far_row})
+    greet(core == 0, {"rows": near_row})
+    beside = jnp.int32(0)
     for axis, me, n in around:
-        @pl.when(me > 0)
-        def _():
-            pl.semaphore_signal(barrier, inc=1, device_id={axis: me - 1}, device_id_type=MESH)
-
-        @pl.when(me < n - 1)
-        def _():
-            pl.semaphore_signal(barrier, inc=1, device_id={axis: me + 1}, device_id_type=MESH)
-
-        greeted = greeted + (me > 0).astype(jnp.int32) + (me < n - 1).astype(jnp.int32)
-    pl.semaphore_wait(barrier, greeted)
-
-    def far_copy(par, c, source):
-        part = pl.ds(c * per_chunk, per_chunk)
+        for there, other in ((me > 0, me - 1), (me < n - 1, me + 1)):
+            greet(there, {"rows": r + 1 - core, axis: other})
+            beside = beside + there.astype(jnp.int32)
+    greeted = has_far.astype(jnp.int32) + core * (1 + 2 * beside)
+
+    @pl.when(greeted > 0)
+    def _():
+        pl.semaphore_wait(barrier, greeted)
+
+    def far_copy(t, p, start, count):
+        par = t % 2
+        source = tracer.at[layer(0), pl.ds(start, count)] if t == 0 else field.at[par, layer(0), pl.ds(1 + start, count)]
         return pltpu.make_async_remote_copy(
-            src_ref=source, dst_ref=far_in.at[par, part],
-            send_sem=far_send.at[par, c], recv_sem=far_recv.at[par, c],
+            src_ref=source, dst_ref=far_in.at[par, pl.ds(start, count)],
+            send_sem=far_send.at[par, p], recv_sem=far_recv.at[par, p],
             device_id={"rows": far_row}, device_id_type=MESH,
         )
-
-    def far_source(par, c):
-        return field.at[par, layer(0), pl.ds(1 + c * per_chunk, per_chunk)]
 
     def near_copy(par, source):
         return pltpu.make_async_remote_copy(
@@ -106,9 +108,18 @@
 
     @pl.when(has_far)
     def _():
-        @pl.loop(0, CHUNKS)
-        def _(c):
-            far_copy(0, c, tracer.at[layer(0), pl.ds(c * per_chunk, per_chunk)]).start()
+        for span in spans(0):
+            far_copy(0, *span).start()
+
+    loads[0].start()
+
+    @pl.when(core == 1)
+    def _():
+        pl.semaphore_signal(all_in, inc=1, device_id={"rows": near_row}, device_id_type=MESH)
+
+    @pl.when(core == 0)
+    def _():
+        pl.semaphore_wait(all_in, 1)
 
     near_copy(0, tracer.at[layer(layers - 1)]).start()
     for side in (0, 1):
@@ -218,19 +229,24 @@
         if not last:
             near_copy(nxt, near_source(nxt)).start()
 
-        @pl.loop(0, CHUNKS)
-        def _(c):
+        if t > 0:
             @pl.when(has_far)
             def _():
-                far_copy(par, c, far_source(par, c)).wait_recv()
-                if t > 0:
-                    far_copy(nxt, c, far_source(nxt, c)).wait_send()
-
-            advance(t, 0, c * per_chunk, per_chunk)
+                for span in spans(t - 1):
+                    far_copy(t - 1, *span).wait_send()
+
+        for p, start, count in spans(t):
+            @pl.when(has_far)
+            def _():
+                far_copy(t, p, start, count).wait_recv()
+
+            advance(t, 0, start, count)
             if not last:
                 @pl.when(has_far)
                 def _():
-                    far_copy(nxt, c, far_source(nxt, c)).start()
+                    for span in spans(t + 1):
+                        if start < span[1] + span[2] <= start + count:
+                            far_copy(t + 1, *span).start()
         if not last:
             for side in (0, 1):
                 @pl.when(has(q, cols_n, side))
@@ -254,9 +270,8 @@
 
     @pl.when(has_far)
     def _():
-        @pl.loop(0, CHUNKS)
-        def _(c):
-            far_copy(par, c, far_source(par, c)).wait_send()
+        for span in spans(STEPS - 1):
+            far_copy(STEPS - 1, *span).wait_send()
 
 
 def solution(mesh):
@@ -276,8 +291,9 @@
                 pltpu.VMEM((2, lines, depth, lanes), jnp.float32),
                 pltpu.VMEM((2, 2, layers, lines, lanes), jnp.float32),
                 pltpu.VMEM((2, 2, layers, lines, lanes), jnp.float32),
+                pltpu.SemaphoreType.REGULAR,
                 dma((2,)),
-                dma((2, CHUNKS)), dma((2, CHUNKS)),
+                dma((2, MOST)), dma((2, MOST)),
                 dma((2,)), dma((2,)),
                 dma((2, 2)), dma((2, 2)),
                 dma((2, 2)), dma((2, 2)),

time: 147 us -> 145 us (0.986)
  Pallas kernels: 142 us -> 140 us
    pallas_call x1, Pallas kernels: 142 us -> 140 us  [on_device(): pl.pallas_call(functools.partial(kernel, sizes), out_shape=pltpu.VMEM(tra...]
where the time goes in v2:
time: 145 us
  Pallas kernels  140 us (97%)
  local copies, waits for them, and re-layouts  4.78 us (3%)
    pallas_call x1, Pallas kernels, on_device(): pl.pallas_call(functools.partial(kernel, sizes), out_shape=pltpu.VMEM(tra...  140 us
    unnamed x1, local copies, waits for them, and re-layouts  4.78 us

profile of v2, /device:TPU:1, one launch (start us, length us, event | category | flops | bytes accessed | tf_op | source)
XLA Modules:
  0.0 144.5 jit_solution(14303205369402802575)
XLA Ops:
  0.0 139.7 %shard_map.28 = f32[4,64,96,128]{3,2,1,0:T(8,128)S(1)} custom-call(f32[4,64,96,128]{3,2,1,0:T(8,128)} %tracer.1, f32[4,64,96,128]{3,2,1,0:T(8,128)} %crowding.1), custom_call_target="tpu_custom_call" | custom-call | tf_op jit(solution)/shard_map/pallas_call | solution.py:283
  139.8 4.8 %copy.4 = f32[4,64,96,128]{3,2,1,0:T(8,128)} copy(f32[4,64,96,128]{3,2,1,0:T(8,128)S(1)} %shard_map.28) | data formatting | bytes 25165824

commit v3 on v2

--- a/solution.py
+++ b/solution.py
@@ -8,7 +8,7 @@
 from jax.sharding import PartitionSpec as P
 
 STEPS = 4
-PARTS = ((32, 32), (32, 32), (32, 32), (32, 16, 8, 6, 2))
+PARTS = ((16, 32, 16), (16, 32, 16), (16, 32, 16), (16, 32, 10, 4, 1, 1))
 MOST = max(map(len, PARTS))
 MESH = pl.DeviceIdType.MESH
 VMEM_LIMIT = 48 * 1024 * 1024
@@ -54,19 +54,6 @@
         def _():
             pl.semaphore_signal(barrier, inc=1, device_id=target, device_id_type=MESH)
 
-    greet(has_far, {"rows": far_row})
-    greet(core == 0, {"rows": near_row})
-    beside = jnp.int32(0)
-    for axis, me, n in around:
-        for there, other in ((me > 0, me - 1), (me < n - 1, me + 1)):
-            greet(there, {"rows": r + 1 - core, axis: other})
-            beside = beside + there.astype(jnp.int32)
-    greeted = has_far.astype(jnp.int32) + core * (1 + 2 * beside)
-
-    @pl.when(greeted > 0)
-    def _():
-        pl.semaphore_wait(barrier, greeted)
-
     def far_copy(t, p, start, count):
         par = t % 2
         source = tracer.at[layer(0), pl.ds(start, count)] if t == 0 else field.at[par, layer(0), pl.ds(1 + start, count)]
@@ -106,10 +93,31 @@
     def has(me, n, side):
         return me > 0 if side == 0 else me < n - 1
 
-    @pl.when(has_far)
-    def _():
+    def open_far():
         for span in spans(0):
             far_copy(0, *span).start()
+
+    greet(has_far, {"rows": far_row})
+    greet(core == 0, {"rows": near_row})
+
+    @pl.when(jnp.logical_and(core == 0, has_far))
+    def _():
+        pl.semaphore_wait(barrier, 1)
+        open_far()
+
+    beside = jnp.int32(0)
+    for axis, me, n in around:
+        for there, other in ((me > 0, me - 1), (me < n - 1, me + 1)):
+            greet(there, {"rows": r + 1 - core, axis: other})
+            beside = beside + there.astype(jnp.int32)
+
+    @pl.when(core == 1)
+    def _():
+        pl.semaphore_wait(barrier, 1 + has_far.astype(jnp.int32) + 2 * beside)
+
+        @pl.when(has_far)
+        def _():
+            open_far()
 
     loads[0].start()
 

time: 145 us -> 145 us (level)
  no operation moved by 1% of the time
where the time goes in v3:
time: 145 us
  Pallas kernels  140 us (97%)
  local copies, waits for them, and re-layouts  4.78 us (3%)
    pallas_call x1, Pallas kernels, on_device(): pl.pallas_call(functools.partial(kernel, sizes), out_shape=pltpu.VMEM(tra...  140 us
    unnamed x1, local copies, waits for them, and re-layouts  4.78 us

profile of v3, /device:TPU:1, one launch (start us, length us, event | category | flops | bytes accessed | tf_op | source)
XLA Modules:
  0.0 144.5 jit_solution(2059551000963270372)
XLA Ops:
  0.0 139.8 %shard_map.28 = f32[4,64,96,128]{3,2,1,0:T(8,128)S(1)} custom-call(f32[4,64,96,128]{3,2,1,0:T(8,128)} %tracer.1, f32[4,64,96,128]{3,2,1,0:T(8,128)} %crowding.1), custom_call_target="tpu_custom_call" | custom-call | tf_op jit(solution)/shard_map/pallas_call | solution.py:291
  139.8 4.8 %copy.4 = f32[4,64,96,128]{3,2,1,0:T(8,128)} copy(f32[4,64,96,128]{3,2,1,0:T(8,128)S(1)} %shard_map.28) | data formatting | bytes 25165824

commit v4 on v3

--- a/solution.py
+++ b/solution.py
@@ -129,7 +129,6 @@
     def _():
         pl.semaphore_wait(all_in, 1)
 
-    near_copy(0, tracer.at[layer(layers - 1)]).start()
     for side in (0, 1):
         @pl.when(has(q, cols_n, side))
         def _():
@@ -169,6 +168,7 @@
         @pl.when(has(s, slabs_n, side))
         def _():
             slab_copy(0, side).start()
+    near_copy(0, tracer.at[layer(layers - 1)]).start()
     loads[1].wait()
 
     row = lax.broadcasted_iota(jnp.int32, (8, 128), 0)
@@ -210,10 +210,21 @@
                     if k == tiles - 1:
                         slab_out[1 - par, 1, here, pl.ds(j, 1), :] = new[7:8]
 
+    def settle():
+        par = (STEPS - 1) % 2
+        near_copy(par, near_source(par)).wait_send()
+        for side in (0, 1):
+            @pl.when(has(q, cols_n, side))
+            def _():
+                cols_copy(par, side, cols_source(par, side)).wait_send()
+
+            @pl.when(has(s, slabs_n, side))
+            def _():
+                slab_copy(par, side).wait_send()
+
     for t in range(STEPS):
         par, last = t % 2, t == STEPS - 1
         nxt = 1 - par
-        near_copy(par, near_source(par)).wait_recv()
         for side in (0, 1):
             @pl.when(has(q, cols_n, 1 - side))
             def _():
@@ -232,7 +243,9 @@
                 @pl.when(has(s, slabs_n, side))
                 def _():
                     slab_copy(nxt, side).wait_send()
-        for d in range(layers - 1, 0, -1):
+        for d in range(1, layers):
+            if d == layers - 1:
+                near_copy(par, near_source(par)).wait_recv()
             advance(t, d, 0, lines)
         if not last:
             near_copy(nxt, near_source(nxt)).start()
@@ -242,6 +255,9 @@
             def _():
                 for span in spans(t - 1):
                     far_copy(t - 1, *span).wait_send()
+
+        if last:
+            settle()
 
         for p, start, count in spans(t):
             @pl.when(has_far)
@@ -265,21 +281,21 @@
                 def _():
                     slab_copy(nxt, side).start()
 
-    par = (STEPS - 1) % 2
-    near_copy(par, near_source(par)).wait_send()
-    for side in (0, 1):
-        @pl.when(has(q, cols_n, side))
-        def _():
-            cols_copy(par, side, cols_source(par, side)).wait_send()
-
-        @pl.when(has(s, slabs_n, side))
-        def _():
-            slab_copy(par, side).wait_send()
-
     @pl.when(has_far)
     def _():
         for span in spans(STEPS - 1):
             far_copy(STEPS - 1, *span).wait_send()
+
+
+def flush(source, out, sem):
+    copies = [
+        pltpu.make_async_copy(source.at[i, pl.ds(h, 32)], out.at[i, pl.ds(h, 32)], sem.at[i, h // 32])
+        for i in range(source.shape[0]) for h in range(0, source.shape[1], 32)
+    ]
+    for copy in copies:
+        copy.start()
+    for copy in copies:
+        copy.wait()
 
 
 def solution(mesh):
@@ -288,7 +304,7 @@
     def on_device(tracer, crowding):
         layers, lines, depth, lanes = tracer.shape
         dma = pltpu.SemaphoreType.DMA
-        return pl.pallas_call(
+        result = pl.pallas_call(
             functools.partial(kernel, sizes),
             out_shape=pltpu.VMEM(tracer.shape, jnp.float32),
             in_specs=[pl.BlockSpec(memory_space=pl.ANY)] * 2,
@@ -310,6 +326,14 @@
                 collective_id=0, has_side_effects=True, vmem_limit_bytes=VMEM_LIMIT,
             ),
         )(tracer, crowding)
+        return pl.pallas_call(
+            flush,
+            out_shape=jax.ShapeDtypeStruct(tracer.shape, jnp.float32),
+            in_specs=[pl.BlockSpec(memory_space=pltpu.VMEM)],
+            out_specs=pl.BlockSpec(memory_space=pl.ANY),
+            scratch_shapes=[dma((layers, lines // 32))],
+            compiler_params=pltpu.CompilerParams(vmem_limit_bytes=1024 * 1024),
+        )(pltpu.with_memory_space_constraint(result, pltpu.VMEM))
 
     placed = P("rows", "cols", "slabs", None)
     return jax.shard_map(on_device, mesh=mesh, in_specs=(placed, placed), out_specs=placed, check_vma=False)

time: 145 us -> 145 us (level)
  local copies, waits for them, and re-layouts: 4.78 us -> 0 us
  Pallas kernels: 140 us -> 144 us
    unnamed x1 -> x0, local copies, waits for them, and re-layouts: 4.78 us -> none
    pallas_call x0 -> x1, Pallas kernels: none -> 4.66 us  [on_device(): pl.pallas_call(flush, out_shape=jax.ShapeDtypeStruct(tracer.shape, jnp.fl...]
where the time goes in v4:
time: 145 us; the launch traced here: 144 us
  Pallas kernels  144 us (99%)
    pallas_call x1, Pallas kernels, on_device(): pl.pallas_call(functools.partial(kernel, sizes), out_shape=pltpu.VMEM(tra...  140 us
    pallas_call x1, Pallas kernels, on_device(): pl.pallas_call(flush, out_shape=jax.ShapeDtypeStruct(tracer.shape, jnp.fl...  4.66 us

profile of v4, /device:TPU:1, one launch (start us, length us, event | category | flops | bytes accessed | tf_op | source)
XLA Modules:
  0.0 144.4 jit_solution(9983414175579387373)
XLA Ops:
  0.0 139.8 %shard_map.28.source = f32[4,64,96,128]{3,2,1,0:T(8,128)S(1)} custom-call(f32[4,64,96,128]{3,2,1,0:T(8,128)} %tracer.1, f32[4,64,96,128]{3,2,1,0:T(8,128)} %crowding.1), custom_call_target="tpu_custom_call" | custom-call | tf_op jit(solution)/shard_map/pallas_call | solution.py:307
  139.8 4.7 %shard_map.29 = f32[4,64,96,128]{3,2,1,0:T(8,128)} custom-call(f32[4,64,96,128]{3,2,1,0:T(8,128)S(1)} %shard_map.28.source), custom_call_target="tpu_custom_call" | custom-call | tf_op jit(solution)/shard_map/pallas_call | solution.py:329

commit v5 on v3

--- a/solution.py
+++ b/solution.py
@@ -129,11 +129,6 @@
     def _():
         pl.semaphore_wait(all_in, 1)
 
-    near_copy(0, tracer.at[layer(layers - 1)]).start()
-    for side in (0, 1):
-        @pl.when(has(q, cols_n, side))
-        def _():
-            cols_copy(0, side, tracer.at[:, (lines - 1) * side]).start()
     loads[1].start()
 
     for side in (0, 1):
@@ -157,6 +152,10 @@
                 far_in[par, j] = jnp.zeros((depth, 128), jnp.float32)
 
     loads[0].wait()
+    for side in (0, 1):
+        @pl.when(has(q, cols_n, side))
+        def _():
+            cols_copy(0, side, tracer.at[:, (lines - 1) * side]).start()
 
     @pl.loop(0, layers)
     def _(i):
@@ -169,6 +168,7 @@
         @pl.when(has(s, slabs_n, side))
         def _():
             slab_copy(0, side).start()
+    near_copy(0, tracer.at[layer(layers - 1)]).start()
     loads[1].wait()
 
     row = lax.broadcasted_iota(jnp.int32, (8, 128), 0)
@@ -213,7 +213,6 @@
     for t in range(STEPS):
         par, last = t % 2, t == STEPS - 1
         nxt = 1 - par
-        near_copy(par, near_source(par)).wait_recv()
         for side in (0, 1):
             @pl.when(has(q, cols_n, 1 - side))
             def _():
@@ -232,7 +231,9 @@
                 @pl.when(has(s, slabs_n, side))
                 def _():
                     slab_copy(nxt, side).wait_send()
-        for d in range(layers - 1, 0, -1):
+        for d in range(1, layers):
+            if d == layers - 1:
+                near_copy(par, near_source(par)).wait_recv()
             advance(t, d, 0, lines)
         if not last:
             near_copy(nxt, near_source(nxt)).start()

time: 145 us -> 145 us (level)
  no operation moved by 1% of the time
where the time goes in v5:
time: 145 us
  Pallas kernels  140 us (97%)
  local copies, waits for them, and re-layouts  4.78 us (3%)
    pallas_call x1, Pallas kernels, on_device(): pl.pallas_call(functools.partial(kernel, sizes), out_shape=pltpu.VMEM(tra...  140 us
    unnamed x1, local copies, waits for them, and re-layouts  4.78 us

profile of v5, /device:TPU:1, one launch (start us, length us, event | category | flops | bytes accessed | tf_op | source)
XLA Modules:
  0.0 144.5 jit_solution(3852370814192672732)
XLA Ops:
  0.0 139.8 %shard_map.28 = f32[4,64,96,128]{3,2,1,0:T(8,128)S(1)} custom-call(f32[4,64,96,128]{3,2,1,0:T(8,128)} %tracer.1, f32[4,64,96,128]{3,2,1,0:T(8,128)} %crowding.1), custom_call_target="tpu_custom_call" | custom-call | tf_op jit(solution)/shard_map/pallas_call | solution.py:292
  139.8 4.8 %copy.4 = f32[4,64,96,128]{3,2,1,0:T(8,128)} copy(f32[4,64,96,128]{3,2,1,0:T(8,128)S(1)} %shard_map.28) | data formatting | bytes 25165824
